TPU v7x, 256 devices: a whole 4x4x8 slice. The times are simulated.
256 devices in a mesh: tm: 64 (over x, z, core), lev: 4 (over y).
Axes of the slice: x: 4, y: 4, z: 8, core: 2. Of those that a mesh axis runs over, the one named last changes fastest.
Arguments:
- fields: bfloat16 [4, 256, 72, 16384], P('lev', 'tm'), may hold values from -18 to 18
- lengths: int32 [64], P('tm'), may hold values from 1 to 4, 192 in all
- owners: int32 [72], replicated, may hold values from 0 to 63, as said below
- thickness: float32 [4], replicated, may hold values from 0.2 to 5
Outputs:
- daily_means: float32 [4, 128, 8, 16384], P('lev', 'tm')
- column_means: float32 [128, 8, 16384], P('tm', None, 'lev')
Inputs may be any that keep to these rules, and one draw needn't show every extreme that they name: `lengths`: the entries sum to 192 and the largest is exactly 4. `owners`: no index owns more than 2 tiles; some index owns exactly 2.
All inputs are finite; a program needn't handle non-finite values. No bound on the sum of `lengths` on one device may be relied on, other than what follows from the above.
Results may differ from a plain program's by a relative error of at most 0.0003.
Values may be sent and summed in bfloat16 or wider, within the bound.
A program may use at most 128 MiB of HBM per device.

v0:
```python
import jax
import jax.numpy as jnp
from jax import lax
from jax.sharding import PartitionSpec as P

MAXT = 2
HOURS_DEV = 3


def laid_out(tiles, dim):
    shape = list(tiles.shape[1:])
    shape[dim] *= tiles.shape[0]
    return jnp.moveaxis(tiles, 0, dim).reshape(shape)


def sent_to_all(value, axis):
    copies = jnp.broadcast_to(value, (lax.axis_size(axis), *value.shape))
    return lax.all_to_all(copies, axis, split_axis=0, concat_axis=0, tiled=True)


def collect(value, axis, dim):
    return laid_out(sent_to_all(value, axis), dim)


def in_blocks(value, dim, devices):
    shape = value.shape
    tiles = value.reshape(*shape[:dim], devices, shape[dim] // devices, *shape[dim + 1 :])
    return jnp.moveaxis(tiles, dim, 0)


def summed_on_arrival(value, axis, dim):
    devices = lax.axis_size(axis)
    tiles = lax.all_to_all(in_blocks(value, dim, devices), axis, 0, 0, tiled=True)
    return jnp.sum(tiles, axis=0)


def slot_table(owners, slot_total):
    tile_count = owners.shape[0]
    tile_ids = jnp.arange(tile_count, dtype=jnp.int32)
    earlier = (owners[None, :] == owners[:, None]) & (tile_ids[None, :] < tile_ids[:, None])
    tile_rank = jnp.sum(earlier.astype(jnp.int32), axis=1)
    position = owners * MAXT + tile_rank
    slot_ids = jnp.arange(slot_total, dtype=jnp.int32)
    matches = (position[None, :] == slot_ids[:, None]).astype(jnp.int32)
    tile_of = jnp.sum(matches * tile_ids[None, :], axis=1)
    slot_valid = jnp.sum(matches, axis=1)
    return (tile_of, slot_valid)


def local(fields, lengths, owners, thickness):
    local_block = fields[0]
    slot_count = local_block.shape[0]
    devices = lax.axis_size("tm")
    my_index = lax.axis_index("tm")
    all_lengths = collect(lengths, "tm", 0)
    offsets = jnp.cumsum(all_lengths) - all_lengths
    tile_of, slot_valid = slot_table(owners, devices * MAXT)
    own_slots = lax.dynamic_slice_in_dim(slot_valid, my_index * MAXT, MAXT, 0).astype(jnp.float32)
    day_ids = jnp.arange(devices * HOURS_DEV // 24, dtype=jnp.int32)
    row_ids = jnp.arange(devices * slot_count, dtype=jnp.int32)
    source_ids = row_ids // slot_count
    slot_ids = row_ids % slot_count
    hour_of = offsets[source_ids] + slot_ids
    is_valid = slot_ids < all_lengths[source_ids]
    select = (is_valid[:, None] & (hour_of[:, None] // 24 == day_ids[None, :])).astype(jnp.bfloat16)
    outgoing = jnp.take(local_block, tile_of, axis=1)
    period_means = (
        jnp.einsum(
            "rd,rmc->mdc",
            select,
            lax.all_to_all(outgoing, "tm", split_axis=1, concat_axis=0, tiled=True),
            preferred_element_type=jnp.float32,
        )
        / 24.0
    )
    period_means = period_means * own_slots[:, None, None]
    my_level = lax.axis_index("lev")
    fraction = thickness[my_level] / jnp.sum(thickness)
    weighted = fraction * period_means
    column_part = summed_on_arrival(weighted, "lev", 2)
    return (period_means[None], column_part)


def solution(mesh):
    placed = (P("lev", "tm", None, None), P("tm"), P(), P())
    return jax.shard_map(
        local,
        mesh=mesh,
        in_specs=placed,
        out_specs=(P("lev", "tm", None, None), P("tm", None, "lev")),
        check_vma=False,
    )
```

profile of v0, /device:TPU:1, one launch (start us, length us, event | category | flops | bytes accessed | tf_op | source)
XLA Modules:
  0.0 503.3 jit_solution(8507707055327906108)
XLA Ops:
  1.3 0.6 broadcast_in_dim.13
  1.9 13.0 %all-to-all-start.1 = ((s32[64,1,1]{2,1,0:T(1,128)}), s32[64,1,1]{2,1,0:T(1,128)S(1)}, u32[]{:S(2)}, u32[]{:S(2)}) async-start(s32[64,1,1]{2,1,0:T(1,128)} %broadcast_in_dim.13), calls=%async_computation.1 | async-start | bytes 65536 | tf_op jit(solution)/shard_map/all_to_all | solution.py:18
  14.9 0.9 convert_reduce_fusion.1
  15.8 0.7 multiply_add_fusion
  16.5 0.1 convert_reduce_fusion
  16.6 13.4 %copy.27 = bf16[1,4,72,16384]{3,1,2,0:T(4,128)(2,1)} copy(bf16[1,4,72,16384]{3,2,1,0:T(8,128)(2,1)} %param.4) | data formatting | bytes 18874368 | tf_op args[0]
  30.0 20.6 %gather_fusion = bf16[128,4,16384]{2,1,0:T(4,128)(2,1)} fusion(bf16[4,72,16384]{2,0,1:T(4,128)(2,1)} %bitcast.34, s32[1024]{0:T(1024)S(1)} %pad_clamp_fusion.1), kind=kCustom, calls=%fused_computation | custom fusion | bytes 33554944 | tf_op jit(solution)/shard_map/jit(_take)/gather | solution.py:66
  50.6 12.2 %select_bitcast_fusion = bf16[4,128,16384]{2,0,1:T(4,128)(2,1)} fusion(bf16[128,4,16384]{2,1,0:T(4,128)(2,1)} %gather_fusion, pred[128]{0:T(512)(128)(4,1)S(1)} %compare_and_fusion), kind=kLoop, calls=%fused_computation.5 | loop fusion | flops 8388608 | bytes 33554560 | tf_op jit(solution)/shard_map/jit(_take)/select_n | solution.py:66
  62.8 10.5 %all-to-all-start = ((bf16[4,128,16384]{2,0,1:T(4,128)(2,1)}), bf16[4,128,16384]{2,0,1:T(4,128)(2,1)}, u32[]{:S(2)}, u32[]{:S(2)}) async-start(bf16[4,128,16384]{2,0,1:T(4,128)(2,1)} %select_bitcast_fusion), calls=%async_computation | async-start | bytes 33554432 | tf_op jit(solution)/shard_map/all_to_all | solution.py:71
  73.4 0.6 dynamic_slice.7
  73.9 0.6 reduce_sum.51
  75.9 0.1 convert_multiply_fusion
  76.0 0.1 reduce-window.9
  76.1 0.1 reduce.1
  76.2 1.2 reduce
  77.4 1.9 gather_fusion.1
  79.3 1.9 gather_fusion.2
  81.2 357.6 %all-to-all-done = bf16[4,128,16384]{2,0,1:T(4,128)(2,1)} async-done(((bf16[4,128,16384]{2,0,1:T(4,128)(2,1)}), bf16[4,128,16384]{2,0,1:T(4,128)(2,1)}, u32[]{:S(2)}, u32[]{:S(2)}) %all-to-all-start) | async-done | bytes 16777248 | tf_op jit(solution)/shard_map/all_to_all | solution.py:71
  438.8 12.0 %copy.26 = bf16[4,64,2,16384]{3,0,1,2:T(4,128)(2,1)} copy(bf16[4,64,2,16384]{3,0,2,1:T(4,128)(2,1)} %bitcast.4) | data formatting | bytes 33554432 | tf_op jit(solution)/shard_map/all_to_all | solution.py:71
  450.8 23.7 %all_to_all.23 = bf16[256,2,16384]{2,0,1:T(8,128)(2,1)} reshape(bf16[64,4,2,16384]{3,1,0,2:T(4,128)(2,1)} %bitcast.35) | data formatting | bytes 33554432 | tf_op jit(solution)/shard_map/all_to_all | solution.py:71
  474.5 9.0 %bitcast_multiply_fusion = (f32[2,8,16384]{2,1,0:T(8,128)S(1)}, f32[2,16384,8]{1,2,0:T(8,128)}) fusion(f32[]{:T(128)S(6)} %div.29, f32[2]{0:T(128)S(1)} %convert_multiply_fusion, bf16[256,2,16384]{2,0,1:T(8,128)(2,1)} %all_to_all.23, s32[256]{0:T(256)S(1)} %and_select_fusion.1, pred[256]{0:T(512)(128)(4,1)S(1)} %fusion.7), kind=kOutput, calls=%fused_computation.7 | convolution fusion | flops 134746112 | bytes 18875660 | tf_op jit(solution)/shard_map/rd,rmc->mdc/dot_general | solution.py:68
  483.6 0.1 copy.28
  483.6 18.9 %all_to_all.29 = f32[4,2,8,4096]{3,2,1,0:T(8,128)S(1)} all-to-all(f32[4,2,8,4096]{3,2,1,0:T(8,128)S(1)} %bitcast.37), channel_id=1, replica_groups=mesh['tm'=64,'lev'=4] {'lev'}, dimensions={0} | all-to-all | bytes 2097152 | tf_op jit(solution)/shard_map/all_to_all | solution.py:33
  502.6 0.8 reduce_sum.52
  (11 shorter events, 0.1 us)
Async XLA Ops:
  1.9 60.9 %all-to-all-start.1 = ((s32[64,1,1]{2,1,0:T(1,128)}), s32[64,1,1]{2,1,0:T(1,128)S(1)}, u32[]{:S(2)}, u32[]{:S(2)}) async-start(s32[64,1,1]{2,1,0:T(1,128)} %broadcast_in_dim.13), calls=%async_computation.1 | async-start | bytes 65536 | tf_op jit(solution)/shard_map/all_to_all | solution.py:18
  62.8 10.5 %copy-start = (f32[4]{0:T(128)S(1)}, f32[4]{0:T(128)}, u32[]{:S(2)}) copy-start(f32[4]{0:T(128)} %param.7) | copy-start | bytes 52
  62.8 376.0 %all-to-all-start = ((bf16[4,128,16384]{2,0,1:T(4,128)(2,1)}), bf16[4,128,16384]{2,0,1:T(4,128)(2,1)}, u32[]{:S(2)}, u32[]{:S(2)}) async-start(bf16[4,128,16384]{2,0,1:T(4,128)(2,1)} %select_bitcast_fusion), calls=%async_computation | async-start | bytes 33554432 | tf_op jit(solution)/shard_map/all_to_all | solution.py:71
where the time goes:
time: 504 us; the launch traced here: 503 us
  waiting for transfers between devices  358 us (71%)
  local copies, waits for them, and re-layouts  74.7 us (15%)
  starting transfers between devices  23.5 us (5%)
  blocking collectives  18.9 us (4%)
  other arithmetic  16.8 us (3%)
  matrix products  9.02 us (2%)
    all_to_all x1, waiting for transfers between devices, local(): lax.all_to_all(outgoing, 'tm', split_axis=1, concat_axis=0, tiled=True)  358 us
    all_to_all x2, local copies, waits for them, and re-layouts, local(): lax.all_to_all(outgoing, 'tm', split_axis=1, concat_axis=0, tiled=True)  35.7 us
    gather x1, local copies, waits for them, and re-layouts, local(): outgoing = jnp.take(local_block, tile_of, axis=1)  20.6 us
    all_to_all x1, blocking collectives, summed_on_arrival(): lax.all_to_all(in_blocks(value, dim, devices), axis, 0, 0, tiled=True)  18.9 us
    unnamed x3, local copies, waits for them, and re-layouts  13.4 us
    all_to_all x1, starting transfers between devices, sent_to_all(): return lax.all_to_all(copies, axis, split_axis=0, concat_axis=0, tiled=True)  13 us
    select_n x2, other arithmetic, local(): outgoing = jnp.take(local_block, tile_of, axis=1)  12.2 us
    all_to_all x1, starting transfers between devices, local(): lax.all_to_all(outgoing, 'tm', split_axis=1, concat_axis=0, tiled=True)  10.5 us
  transfers between devices with their start and end apart: 2, of which 1 were waited for; matrix products, arithmetic and copies ran while one was open for 11% of the time, Pallas kernels for 0%

commit v1 on v0

v1 whole, which is shorter than its diff:
```python
import jax
import jax.numpy as jnp
from jax import lax
from jax.experimental import pallas as pl
from jax.experimental.pallas import tpu as pltpu
from jax.sharding import PartitionSpec as P

MESH = pl.DeviceIdType.MESH
MAXT = 2
CAP = 4
TILES = 72
CELLS = 16384
NX, NZ, NC, NY = 4, 8, 2, 4
N_TM = NX * NZ * NC
DAYS = 8
CH = CELLS // (NZ * NC)
HALF = CELLS // NC
GROUPS = TILES // 8
XSLOTS = 4
ZW = GROUPS * CH + 128
FW = CH + 128
TOP = 32700.0
FINE = 256.0


def far_first(n):
    k = (n + 1) // 2
    return lax.rem(4 + k * (2 * lax.rem(n, 2) - 1) + 8, 8)


def code_of(peak):
    return jnp.ceil(jnp.log(jnp.maximum(peak, 1e-30)) * FINE)


def kernel(fields, wz, cz, frac, pick, spread, daily, column,
           own, other, zf32, zbuf, acc, fbuf, lsend, lrecv,
           own_sem, pair_send, pair_recv, z_send, z_recv, f_send, f_recv, l_send, l_recv):
    me = lax.axis_index("tm")
    my_y = lax.axis_index("lev")
    core = lax.rem(me, NC)
    my_z = lax.rem(me // NC, NZ)
    my_x = me // (NC * NZ)
    partner = me + 1 - 2 * core

    def own_copy(n):
        lanes = pl.multiple_of(core * HALF + lax.rem(my_z + far_first(n), NZ) * CH, CH)
        return pltpu.make_async_copy(
            fields.at[0, :, :, pl.ds(lanes, CH)], own.at[n], own_sem.at[n])

    def pair_copy(n):
        lanes = pl.multiple_of((1 - core) * HALF + lax.rem(my_z + far_first(n), NZ) * CH, CH)
        return pltpu.make_async_remote_copy(
            src_ref=fields.at[0, :, :, pl.ds(lanes, CH)], dst_ref=other.at[n],
            send_sem=pair_send.at[n], recv_sem=pair_recv.at[n],
            device_id=(partner, my_y), device_id_type=MESH)

    def start_own(n, carry):
        own_copy(n).start()
        return carry

    lax.fori_loop(0, NZ, start_own, 0)

    barrier = pltpu.get_barrier_semaphore()

    def greet_tm(r, carry):
        pl.semaphore_signal(barrier, inc=1, device_id=(lax.rem(me + r, N_TM), my_y), device_id_type=MESH)
        return carry

    def greet_lev(r, carry):
        pl.semaphore_signal(barrier, inc=1, device_id=(me, lax.rem(my_y + r, NY)), device_id_type=MESH)
        return carry

    lax.fori_loop(1, N_TM, greet_tm, 0)
    lax.fori_loop(1, NY, greet_lev, 0)
    pl.semaphore_wait(barrier, N_TM - 1 + NY - 1)

    def start_pair(n, carry):
        pair_copy(n).start()
        return carry

    lax.fori_loop(0, NZ, start_pair, 0)

    def z_copy(off):
        target = (my_x * NZ + lax.rem(my_z + off, NZ)) * NC + core
        return pltpu.make_async_remote_copy(
            src_ref=zbuf.at[off], dst_ref=zbuf.at[NZ + off],
            send_sem=z_send.at[off], recv_sem=z_recv.at[off],
            device_id=(target, my_y), device_id_type=MESH)

    def z_out(n, carry):
        off = far_first(n)
        own_copy(n).wait()
        pair_copy(n).wait_recv()

        def sums(g, peak):
            rows = pl.ds(pl.multiple_of(g * 8, 8), 8)
            first = jnp.zeros((8, CH), jnp.float32)
            second = jnp.zeros((8, CH), jnp.float32)
            for part, ref in enumerate((own, other)):
                for j in range(CAP):
                    hour = ref[n, j, rows, :].astype(jnp.float32)
                    first += wz[part * 8 + j] * hour
                    second += wz[part * 8 + 4 + j] * hour
            zf32[g, 0:8, :] = first
            zf32[g, 8:16, :] = second
            both = jnp.concatenate([first, second], axis=0)
            for l in range(CH // 128):
                peak = jnp.maximum(peak, jnp.abs(both[:, l * 128:(l + 1) * 128]))
            return peak

        code = code_of(lax.fori_loop(0, GROUPS, sums, jnp.zeros((16, 128), jnp.float32)))
        scale = jnp.exp(code * (-1.0 / FINE)) * TOP
        zbuf[off, :, GROUPS * CH:] = code.astype(jnp.int32).astype(jnp.int16)

        def shrink(g, carry):
            for l in range(CH // 128):
                value = jnp.round(zf32[g, :, l * 128:(l + 1) * 128] * scale)
                at = pl.multiple_of(g * CH + l * 128, 128)
                zbuf[off, :, pl.ds(at, 128)] = value.astype(jnp.int32).astype(jnp.int16)
            return carry

        lax.fori_loop(0, GROUPS, shrink, 0)

        @pl.when(off > 0)
        def _():
            z_copy(off).start()

        return carry

    lax.fori_loop(0, NZ, z_out, 0)

    acc[...] = jnp.zeros_like(acc)

    def z_in(n, carry):
        off = far_first(n)

        @pl.when(off > 0)
        def _():
            z_copy(off).wait_recv()

        at = off + NZ * jnp.minimum(off, 1)
        code = zbuf[at, :, GROUPS * CH:].astype(jnp.int32).astype(jnp.float32)
        scale = jnp.exp(code * (1.0 / FINE)) * (1.0 / TOP)

        def add(g, carry):
            rows = pl.multiple_of(g * 8, 8)
            for l in range(CH // 128):
                lanes = pl.ds(pl.multiple_of(g * CH + l * 128, 128), 128)
                value = zbuf[at, :, lanes].astype(jnp.int32).astype(jnp.float32) * scale
                low, high = value[0:8], value[8:16]
                for s in range(XSLOTS):
                    here = (pl.ds(s * TILES + rows, 8), slice(l * 128, (l + 1) * 128))
                    acc[here] += cz[off * 8 + s] * low + cz[off * 8 + 4 + s] * high
            return carry

        lax.fori_loop(0, GROUPS, add, 0)
        return carry

    lax.fori_loop(0, NZ, z_in, 0)

    def owners_out(b, carry):
        lines = pick[pl.ds(pl.multiple_of(b * 64, 64), 64), :]
        for l in range(CH // 256):
            part = acc[:, l * 256:(l + 1) * 256]
            high = part.astype(jnp.bfloat16)
            rest = part - high.astype(jnp.float32)
            mid = rest.astype(jnp.bfloat16)
            low = (rest - mid.astype(jnp.float32)).astype(jnp.bfloat16)
            got = jnp.dot(lines, high, preferred_element_type=jnp.float32)
            got += jnp.dot(lines, mid, preferred_element_type=jnp.float32)
            got += jnp.dot(lines, low, preferred_element_type=jnp.float32)
            zf32[0:4, :, l * 256:(l + 1) * 256] = got.reshape(4, 16, 256)

        for t in range(8):
            rows = zf32[t // 2, (t % 2) * 8:(t % 2) * 8 + 8, 0:CH]
            peak = jnp.zeros((8, 128), jnp.float32)
            for l in range(CH // 128):
                peak = jnp.maximum(peak, jnp.abs(rows[:, l * 128:(l + 1) * 128]))
            code = code_of(peak)
            scale = jnp.exp(code * (-1.0 / FINE)) * TOP
            fbuf[b * 8 + t, :, CH:] = code.astype(jnp.int32).astype(jnp.int16)
            for l in range(CH // 128):
                value = jnp.round(rows[:, l * 128:(l + 1) * 128] * scale)
                fbuf[b * 8 + t, :, l * 128:(l + 1) * 128] = value.astype(jnp.int32).astype(jnp.int16)
        return carry

    lax.fori_loop(0, N_TM // 8, owners_out, 0)

    def relative(i):
        n, dc, dx = i // 8, lax.rem(i // 4, 2), lax.rem(i, 4)
        return dx, far_first(n), dc

    def f_copy(i):
        dx, dz, dc = relative(i)
        target = (lax.rem(my_x + dx, NX) * NZ + lax.rem(my_z + dz, NZ)) * NC + lax.rem(core + dc, NC)
        return pltpu.make_async_remote_copy(
            src_ref=fbuf.at[target], dst_ref=fbuf.at[N_TM + i],
            send_sem=f_send.at[i], recv_sem=f_recv.at[i],
            device_id=(target, my_y), device_id_type=MESH)

    SELF = N_TM - 8

    def f_start(i, carry):
        @pl.when(i != SELF)
        def _():
            f_copy(i).start()

        return carry

    lax.fori_loop(0, N_TM, f_start, 0)

    def l_copy(piece, to, turn):
        return pltpu.make_async_remote_copy(
            src_ref=lsend.at[piece], dst_ref=lrecv.at[turn, lax.rem(piece, 4)],
            send_sem=l_send.at[piece], recv_sem=l_recv.at[turn, lax.rem(piece, 4)],
            device_id=(me, to), device_id_type=MESH)

    def owners_in(p, carry):
        _, dz, dc = relative(p * 4)
        piece = lax.rem(core + dc, NC) * NZ + lax.rem(my_z - dz + NZ, NZ)
        parts = []
        for dx in range(NX):
            i = p * 4 + dx
            if dx == 0:
                @pl.when(i != SELF)
                def _():
                    f_copy(i).wait_recv()

                alone = jnp.where(i == SELF, 1, 0)
                at = alone * me + (1 - alone) * (N_TM + i)
            else:
                f_copy(i).wait_recv()
                at = N_TM + i
            code = fbuf[at, :, CH:].astype(jnp.int32).astype(jnp.float32)
            scale = jnp.exp(code * (1.0 / FINE)) * (1.0 / TOP)
            value = fbuf[at, :, 0:CH].astype(jnp.int32).astype(jnp.float32)
            parts.append(value * jnp.concatenate([scale] * (CH // 128), axis=1))
        value = jnp.concatenate(parts, axis=0)
        means = jnp.dot(spread[...], value, preferred_element_type=jnp.float32,
                        precision=lax.Precision.HIGHEST) * (1.0 / 24.0)
        lanes = pl.ds(pl.multiple_of(piece * CH, CH), CH)
        daily[0, 0, :, lanes] = means[0:8]
        daily[0, 1, :, lanes] = means[8:16]
        lsend[piece] = means * frac[0]
        to = piece // 4
        turn = lax.rem(to - my_y + NY, NY)

        @pl.when(turn > 0)
        def _():
            l_copy(piece, to, turn).start()

        return carry

    lax.fori_loop(0, NZ * NC, owners_in, 0)

    for s in range(4):
        total = lsend[my_y * 4 + s]
        for turn in range(1, NY):
            l_copy(my_y * 4 + s, my_y, turn).wait_recv()
            total += lrecv[turn, s]
        column[0, :, s * CH:(s + 1) * CH] = total[0:8]
        column[1, :, s * CH:(s + 1) * CH] = total[8:16]

    def drain_pair(n, carry):
        pair_copy(n).wait_send()
        return carry

    def drain_z(off, carry):
        z_copy(off).wait_send()
        return carry

    def drain_f(i, carry):
        @pl.when(i != SELF)
        def _():
            f_copy(i).wait_send()

        return carry

    def drain_l(piece, carry):
        to = piece // 4
        turn = lax.rem(to - my_y + NY, NY)

        @pl.when(turn > 0)
        def _():
            l_copy(piece, to, turn).wait_send()

        return carry

    lax.fori_loop(0, NZ, drain_pair, 0)
    lax.fori_loop(1, NZ, drain_z, 0)
    lax.fori_loop(0, N_TM, drain_f, 0)
    lax.fori_loop(0, NZ * NC, drain_l, 0)


def slot_table(owners, slot_total):
    tile_count = owners.shape[0]
    tile_ids = jnp.arange(tile_count, dtype=jnp.int32)
    earlier = (owners[None, :] == owners[:, None]) & (tile_ids[None, :] < tile_ids[:, None])
    tile_rank = jnp.sum(earlier.astype(jnp.int32), axis=1)
    return owners * MAXT + tile_rank


def local(fields, lengths, owners, thickness):
    me = lax.axis_index("tm")
    core, my_z, my_x = me % NC, (me // NC) % NZ, me // (NC * NZ)
    chip = me // NC
    lens = lax.all_gather(lengths, "tm", axis=0, tiled=True)
    ids = jnp.arange(N_TM, dtype=jnp.int32)
    offsets = jnp.sum(jnp.where(ids[None, :] < ids[:, None], lens[None, :], 0), axis=1)
    chip_day = offsets[::NC] // 24
    plane_day = offsets[:: NC * NZ] // 24
    devs = jnp.stack([me, me + 1 - 2 * core])
    j = jnp.arange(CAP, dtype=jnp.int32)
    slot = (offsets[devs][:, None] + j[None, :]) // 24 - chip_day[chip]
    slot = jnp.where(j[None, :] < lens[devs][:, None], slot, -1)
    wz = (slot[:, None, :] == jnp.arange(2)[None, :, None]).astype(jnp.float32).reshape(16)
    from_z = (my_z - jnp.arange(NZ) + NZ) % NZ
    shift = chip_day[my_x * NZ + from_z] - plane_day[my_x]
    cz = (shift[:, None, None] + jnp.arange(2)[None, :, None] == jnp.arange(XSLOTS)[None, None, :])
    cz = cz.astype(jnp.float32).reshape(NZ * 2 * XSLOTS)
    from_x = (my_x - jnp.arange(NX) + NX) % NX
    rows, cols = jnp.arange(16, dtype=jnp.int32), jnp.arange(32, dtype=jnp.int32)
    day = plane_day[from_x][cols // 8] + cols % 4
    spread = (rows[:, None] // 8 == ((cols // 4) % 2)[None, :]) & (rows[:, None] % 8 == day[None, :])
    spread = spread.astype(jnp.float32)
    position = slot_table(owners, N_TM * MAXT)
    lines = jnp.arange(N_TM * MAXT * XSLOTS, dtype=jnp.int32)
    taken = (position[None, :] == (lines // XSLOTS)[:, None])
    pick = jnp.concatenate(
        [taken & (lines % XSLOTS == s)[:, None] for s in range(XSLOTS)], axis=1).astype(jnp.bfloat16)
    frac = (thickness[lax.axis_index("lev")] / jnp.sum(thickness)).reshape(1)

    dma = pltpu.SemaphoreType.DMA
    daily, column = pl.pallas_call(
        kernel,
        out_shape=(
            jax.ShapeDtypeStruct((1, MAXT, DAYS, CELLS), jnp.float32),
            jax.ShapeDtypeStruct((MAXT, DAYS, CELLS // NY), jnp.float32),
        ),
        in_specs=[
            pl.BlockSpec(memory_space=pl.ANY),
            pl.BlockSpec(memory_space=pltpu.SMEM),
            pl.BlockSpec(memory_space=pltpu.SMEM),
            pl.BlockSpec(memory_space=pltpu.SMEM),
            pl.BlockSpec(memory_space=pltpu.VMEM),
            pl.BlockSpec(memory_space=pltpu.VMEM),
        ],
        out_specs=(pl.BlockSpec(memory_space=pltpu.VMEM), pl.BlockSpec(memory_space=pltpu.VMEM)),
        scratch_shapes=[
            pltpu.VMEM((NZ, CAP, TILES, CH), jnp.bfloat16),
            pltpu.VMEM((NZ, CAP, TILES, CH), jnp.bfloat16),
            pltpu.VMEM((GROUPS, 16, CH), jnp.float32),
            pltpu.VMEM((2 * NZ, 16, ZW), jnp.int16),
            pltpu.VMEM((XSLOTS * TILES, CH), jnp.float32),
            pltpu.VMEM((2 * N_TM, 8, FW), jnp.int16),
            pltpu.VMEM((NZ * NC, 16, CH), jnp.float32),
            pltpu.VMEM((NY, 4, 16, CH), jnp.float32),
            dma((NZ,)), dma((NZ,)), dma((NZ,)), dma((NZ,)), dma((NZ,)),
            dma((N_TM,)), dma((N_TM,)), dma((NZ * NC,)), dma((NY, 4)),
        ],
        compiler_params=pltpu.CompilerParams(collective_id=0, has_side_effects=True),
    )(fields, wz, cz, frac, pick, spread)
    return daily, column


def solution(mesh):
    placed = (P("lev", "tm", None, None), P("tm"), P(), P())
    return jax.shard_map(
        local,
        mesh=mesh,
        in_specs=placed,
        out_specs=(P("lev", "tm", None, None), P("tm", None, "lev")),
        check_vma=False,
    )
```

time: 504 us -> 163 us (0.32)
  waiting for transfers between devices: 358 us -> 0 us
  Pallas kernels: 0 us -> 114 us
  local copies, waits for them, and re-layouts: 74.7 us -> 13.1 us
  starting transfers between devices: 23.5 us -> 0 us
  matrix products: 9.02 us -> 0 us
  other arithmetic: 16.8 us -> 9.66 us
    all_to_all x2 -> x0, waiting for transfers between devices: 358 us -> none  [the longest x1 358 us: local(): lax.all_to_all(outgoing, 'tm', split_axis=1, concat_axis=0, tiled=True)]
    pallas_call x0 -> x1, Pallas kernels: none -> 114 us  [local(): pl.pallas_call(kernel, out_shape=(jax.ShapeDtypeStruct((1, MAXT, DAYS, CE...]
    all_to_all x2 -> x0, local copies, waits for them, and re-layouts: 35.7 us -> none  [local(): lax.all_to_all(outgoing, 'tm', split_axis=1, concat_axis=0, tiled=True)]
    all_to_all x2 -> x0, starting transfers between devices: 23.5 us -> none  [the longest x1 13 us: sent_to_all(): return lax.all_to_all(copies, axis, split_axis=0, concat_axis=0, tiled=True)]
    gather x3 -> x5, local copies, waits for them, and re-layouts: 24.3 us -> 3.17 us  [the longest x2 1.25 us: local(): day = plane_day[from_x][cols // 8] + cols % 4]
    unnamed x0 -> x1, blocking collectives: none -> 20.7 us
    all_to_all x1 -> x0, blocking collectives: 18.9 us -> none  [summed_on_arrival(): lax.all_to_all(in_blocks(value, dim, devices), axis, 0, 0, tiled=True)]
    dot_general x1 -> x0, matrix products: 9.02 us -> none  [local(): jnp.einsum('rd,rmc->mdc', select, lax.all_to_all(outgoing, 'tm', split_ax...]
  transfers between devices with their start and end apart: 2 -> 0, of which waited for: 1 -> 0; matrix products, arithmetic and copies ran while one was open for 11% -> 0% of each run, Pallas kernels for 0% -> 0%
where the time goes in v1:
time: 163 us; the launch traced here: 160 us
  Pallas kernels  114 us (70%)
  blocking collectives  20.7 us (13%)
  local copies, waits for them, and re-layouts  13.1 us (8%)
  other arithmetic  9.66 us (6%)
  between operations  2.77 us (2%)
    pallas_call x1, Pallas kernels, local(): pl.pallas_call(kernel, out_shape=(jax.ShapeDtypeStruct((1, MAXT, DAYS, CE...  114 us
    unnamed x1, blocking collectives  20.7 us
    unnamed x5, local copies, waits for them, and re-layouts  5.95 us

profile of v1, /device:TPU:1, one launch (start us, length us, event | category | flops | bytes accessed | tf_op | source)
XLA Modules:
  0.0 160.3 jit_solution(15518468373112749661)
XLA Ops:
  1.4 1.3 reduce_sum.28
  2.7 1.2 dynamic_slice.11
  5.3 1.3 dynamic-slice
  6.5 0.9 convert_reduce_fusion
  7.5 0.7 multiply_add_fusion
  8.1 0.8 dynamic-update-slice
  8.9 20.7 %all-reduce = s32[64]{0:T(128)S(1)} all-reduce(s32[64]{0:T(128)S(1)} %dynamic-update-slice), channel_id=1, replica_groups=mesh['tm'=64,'lev'=4] {'tm'}, use_global_device_ids=true, to_apply=%add | all-reduce | flops 64 | bytes 512
  29.8 0.6 dynamic_slice.10
  30.5 0.6 dynamic_slice.9
  31.2 0.6 gather_fusion.1
  31.8 0.6 gather_fusion
  32.4 0.7 compare_select_fusion.13
  33.2 0.6 reshape.447.wz
  33.8 0.6 gather_fusion.3
  34.4 0.6 fusion.18
  35.1 2.5 %and_select_fusion.4 = (s32[32]{0:T(128)S(1)}, s32[32]{0:T(128)S(1)}) fusion(s32[]{:T(128)} %bitcast.13, s32[]{:T(128)} %bitcast.12, s32[]{:T(128)} %bitcast.11, s32[]{:T(128)} %bitcast.10), kind=kLoop, calls=%fused_computation.49 | loop fusion | flops 1312 | bytes 272 | tf_op jit(solution)/shard_map/jit(remainder)/select_n | solution.py:324
  37.6 0.6 gather_fusion.2
  38.3 0.7 broadcast_subtract_fusion
  39.1 0.7 reshape.448.cz
  39.8 0.7 and_convert_fusion.spread
  41.0 1.2 add_convert_fusion.pick
  42.2 114.1 %shard_map.59 = (f32[1,2,8,16384]{3,2,1,0:T(8,128)}, f32[2,8,4096]{2,1,0:T(8,128)}) custom-call(bf16[1,4,72,16384]{3,2,1,0:T(8,128)(2,1)} %fields.1, f32[16]{0:T(128)} %reshape.447.wz, f32[64]{0:T(128)} %reshape.448.cz, f32[1]{0:T(128)} %bitcast.8.frac, bf16[512,288]{1,0:T(8,128)(2,1)} %add_convert_fusion.pick, f32[16,32]{1,0:T(8,128)} %and_convert_fusion.spread), custom_call_target="tpu_custom_call" | custom-call | tf_op jit(solution)/shard_map/pallas_call | solution.py:334
  156.3 2.3 %copy.11 = f32[1,2,8,16384]{3,2,1,0:T(8,128)} copy(f32[1,2,8,16384]{3,2,1,0:T(8,128)} %get-tuple-element.20) | data formatting | bytes 2097152
  158.6 1.7 %copy.12 = f32[2,8,4096]{2,1,0:T(8,128)} copy(f32[2,8,4096]{2,1,0:T(8,128)} %get-tuple-element.21) | data formatting | bytes 524288
  (20 shorter events, 1.2 us)

commit v2 on v1

v2 whole, which is shorter than its diff:
```python
import jax
import jax.numpy as jnp
from jax import lax
from jax.experimental import pallas as pl
from jax.experimental.pallas import tpu as pltpu
from jax.sharding import PartitionSpec as P

MESH = pl.DeviceIdType.MESH
MAXT = 2
CAP = 4
TILES = 72
CELLS = 16384
NX, NZ, NC, NY = 4, 8, 2, 4
N_TM = NX * NZ * NC
CHIPS = NX * NZ
DAYS = 8
CH = CELLS // (NZ * NC)
HALF = CELLS // NC
GROUPS = TILES // 8
WIN = 4
SUB = 2
CW = CH // SUB
LONG, SHORT = 4, 3
FW = CH + 128
TOP = 32700.0
FINE = 256.0


def touched(chips):
    return (8 * chips - 2) // 24 + 2


def far_first(n):
    k = (n + 1) // 2
    return lax.rem(4 + k * (2 * lax.rem(n, 2) - 1) + 8, 8)


def code_of(peak):
    return jnp.ceil(jnp.log(jnp.maximum(peak, 1e-30)) * FINE)


def day_of(hour):
    return lax.shift_right_logical(hour * 2731, 16)


def kernel(fields, length, thickness, place, daily, column,
           own, other, lens, offs, pick, zf32, two_out, two_in, three_out, three_in, acc, fbuf, lsend, lrecv,
           own_sem, pair_send, pair_recv, n_send, n_recv, z_send, z_recv, f_send, f_recv, l_send, l_recv):
    me = lax.axis_index("tm")
    my_y = lax.axis_index("lev")
    core = lax.rem(me, NC)
    chip = me // NC
    my_z = lax.rem(chip, NZ)
    my_x = chip // NZ
    partner = me + 1 - 2 * core
    way = 1 - 2 * core

    def chunk_lanes(n, of_core):
        ahead = (1 - lax.rem(n, 2)) * (4 - n // 2) - lax.rem(n, 2) * (3 - n // 2)
        z = lax.rem(my_z + ahead * (1 - 2 * of_core) + NZ, NZ)
        return pl.ds(pl.multiple_of(of_core * HALF + z * CH, CH), CH)

    def own_copy(n):
        return pltpu.make_async_copy(
            fields.at[0, :, :, chunk_lanes(n, core)], own.at[n], own_sem.at[n])

    def pair_copy(n):
        return pltpu.make_async_remote_copy(
            src_ref=fields.at[0, :, :, chunk_lanes(n, 1 - core)], dst_ref=other.at[n],
            send_sem=pair_send.at[n], recv_sem=pair_recv.at[n],
            device_id=(partner, my_y), device_id_type=MESH)

    def start_own(n, carry):
        own_copy(n).start()
        return carry

    lax.fori_loop(0, NZ, start_own, 0)

    barrier = pltpu.get_barrier_semaphore()

    def greet_tm(r, carry):
        pl.semaphore_signal(barrier, inc=1, device_id=(lax.rem(me + r, N_TM), my_y), device_id_type=MESH)
        return carry

    def greet_lev(r, carry):
        pl.semaphore_signal(barrier, inc=1, device_id=(me, lax.rem(my_y + r, NY)), device_id_type=MESH)
        return carry

    lax.fori_loop(1, N_TM, greet_tm, 0)
    lax.fori_loop(1, NY, greet_lev, 0)

    lens[pl.ds(me, 1), :] = jnp.full((1, 128), length[0], jnp.int32)
    width = WIN * TILES
    line = lax.broadcasted_iota(jnp.int32, (MAXT * N_TM * WIN, width), 0)
    lane = lax.broadcasted_iota(jnp.int32, (MAXT * N_TM * WIN, width), 1)
    first_lane = (line & 3) * TILES
    taken = (place[...] == lax.shift_right_logical(line, 2)) & (lane >= first_lane) & (lane < first_lane + TILES)
    pick[...] = jnp.where(taken, 1.0, 0.0).astype(jnp.bfloat16)
    share = jnp.full((16, 128), thickness[my_y], jnp.float32) / jnp.full(
        (16, 128), thickness[0] + thickness[1] + thickness[2] + thickness[3], jnp.float32)

    pl.semaphore_wait(barrier, N_TM - 1 + NY - 1)

    def length_copy(r):
        return pltpu.make_async_remote_copy(
            src_ref=lens.at[pl.ds(me, 1), :], dst_ref=lens.at[pl.ds(me, 1), :],
            send_sem=n_send.at[r], recv_sem=n_recv.at[r],
            device_id=(lax.rem(me + r, N_TM), my_y), device_id_type=MESH)

    def start_length(r, carry):
        length_copy(r).start()
        return carry

    def start_pair(n, carry):
        pair_copy(n).start()
        return carry

    def take_length(r, carry):
        length_copy(r).wait_recv()
        return carry

    lax.fori_loop(0, 2, start_pair, 0)
    lax.fori_loop(1, N_TM, start_length, 0)
    lax.fori_loop(2, NZ, start_pair, 0)
    lax.fori_loop(1, N_TM, take_length, 0)
    before = (lax.broadcasted_iota(jnp.int32, (N_TM, N_TM), 1)
              < lax.broadcasted_iota(jnp.int32, (N_TM, N_TM), 0))
    offs[...] = jnp.dot(
        jnp.where(before, 1.0, 0.0).astype(jnp.bfloat16),
        lens[...].astype(jnp.float32).astype(jnp.bfloat16),
        preferred_element_type=jnp.float32).astype(jnp.int32)

    def day(q):
        q = lax.rem(q + 2 * CHIPS, CHIPS)
        return day_of(jnp.broadcast_to(offs[pl.ds(q * NC, 1), :], (8, 128)))

    my_day = day(chip)

    def hour_weights(device):
        start = jnp.broadcast_to(offs[pl.ds(device, 1), :], (8, 128))
        held = jnp.broadcast_to(lens[pl.ds(device, 1), :], (8, 128))
        slots = [jnp.where(held > j, day_of(start + j) - my_day, -1) for j in range(CAP)]
        return [[jnp.where(slot == i, 1.0, 0.0) for slot in slots] for i in range(2)]

    weights = (hour_weights(me), hour_weights(partner))

    def moves(shift, slots, total):
        return [[jnp.where(shift == s - i, 1.0, 0.0) if s >= i else None for s in range(total)] for i in range(slots)]

    def chip_sums(n, g, lanes):
        rows = pl.ds(pl.multiple_of(g * 8, 8), 8)
        sums = [None, None]
        for part, ref in enumerate((own, other)):
            for j in range(CAP):
                hour = ref[n, j, rows, lanes].astype(jnp.float32)
                for i in range(2):
                    term = weights[part][i][j] * hour
                    sums[i] = term if sums[i] is None else sums[i] + term
        return sums

    def scale_in(buf, units):
        code = buf[:, units * CW:].astype(jnp.int32).astype(jnp.float32)
        return jnp.exp(code * (1.0 / FINE)) * (1.0 / TOP)

    def taken_in(buf, unit, l, scale):
        lanes = pl.ds(pl.multiple_of(unit * CW + l * 128, 128), 128)
        return buf[:, lanes].astype(jnp.int32).astype(jnp.float32) * scale

    def combined(total, sources):
        outs = [None] * total
        for values, table in sources:
            for i, value in enumerate(values):
                for s in range(i, total):
                    term = table[i][s] * value
                    outs[s] = term if outs[s] is None else outs[s] + term
        return outs

    def link(short, n, s):
        at = n - 1 + (LONG if short else 0)
        if n == LONG:
            src, dst = three_out.at[s], three_in.at[s]
        else:
            row = n - 1 + (3 if short else 0)
            src, dst = two_out.at[row, s], two_in.at[row, s]
        to = lax.rem(chip + (-way if short else way) + CHIPS, CHIPS)
        return pltpu.make_async_remote_copy(
            src_ref=src, dst_ref=dst, send_sem=z_send.at[at, s], recv_sem=z_recv.at[at, s],
            device_id=(to * NC + core, my_y), device_id_type=MESH)

    def arrived(short, n, s):
        if n == LONG:
            return three_in.at[s]
        return two_in.at[n - 1 + (3 if short else 0), s]

    def forward(short, n):
        at = 2 * n - 1 if short else 2 * (n - 1)
        own_copy(at).wait()
        pair_copy(at).wait_recv()
        rising = core if short else 1 - core
        first = chip - (n - 1) * rising
        base = day(first)
        total = touched(n)
        mine = moves((my_day - base) & 7, 2, total)
        if n > 1:
            theirs = moves((day(first + 1 - rising) - base) & 7, 2, total)

        def part(s, carry):
            if n > 1:
                link(short, n - 1, s).wait_recv()
                source = arrived(short, n - 1, s)
                scale = scale_in(source, 2 * GROUPS)

            def sums(g, peak):
                for l in range(CW // 128):
                    lanes = pl.ds(pl.multiple_of(s * CW + l * 128, 128), 128)
                    sources = [(chip_sums(at, g, lanes), mine)]
                    if n > 1:
                        sources.append(([taken_in(source, i * GROUPS + g, l, scale) for i in range(2)], theirs))
                    for i, value in enumerate(combined(total, sources)):
                        zf32[i * GROUPS + g, :, l * 128:(l + 1) * 128] = value
                        peak = jnp.maximum(peak, jnp.abs(value))
                return peak

            code = code_of(lax.fori_loop(0, GROUPS, sums, jnp.zeros((8, 128), jnp.float32)))
            down = jnp.exp(code * (-1.0 / FINE)) * TOP
            out = three_out.at[s] if n == LONG else two_out.at[n - 1 + (3 if short else 0), s]
            out[:, total * GROUPS * CW:] = code.astype(jnp.int32).astype(jnp.int16)

            def shrink(u, carry):
                for l in range(CW // 128):
                    value = jnp.round(zf32[u, :, l * 128:(l + 1) * 128] * down)
                    lanes = pl.ds(pl.multiple_of(u * CW + l * 128, 128), 128)
                    out[:, lanes] = value.astype(jnp.int32).astype(jnp.int16)
                return carry

            lax.fori_loop(0, total * GROUPS, shrink, 0)
            link(short, n, s).start()
            return carry

        lax.fori_loop(0, SUB, part, 0)

    for n in range(1, LONG + 1):
        forward(False, n)
        if n <= SHORT:
            forward(True, n)

    own_copy(NZ - 1).wait()
    pair_copy(NZ - 1).wait_recv()
    base = day(chip - (LONG - core))
    mine = moves((my_day - base) & 7, 2, WIN)
    long_day = day(chip - LONG + core * (LONG + 1))
    short_day = day(chip + 1 - core * (SHORT + 1))
    from_long = moves((long_day - base) & 7, touched(LONG), WIN)
    from_short = moves((short_day - base) & 7, touched(SHORT), WIN)

    def window(s, carry):
        link(False, LONG, s).wait_recv()
        link(True, SHORT, s).wait_recv()
        far, near = arrived(False, LONG, s), arrived(True, SHORT, s)
        far_scale = scale_in(far, touched(LONG) * GROUPS)
        near_scale = scale_in(near, touched(SHORT) * GROUPS)

        def add(g, carry):
            for l in range(CW // 128):
                lanes = pl.ds(pl.multiple_of(s * CW + l * 128, 128), 128)
                outs = combined(WIN, [
                    (chip_sums(NZ - 1, g, lanes), mine),
                    ([taken_in(far, i * GROUPS + g, l, far_scale) for i in range(touched(LONG))], from_long),
                    ([taken_in(near, i * GROUPS + g, l, near_scale) for i in range(touched(SHORT))], from_short),
                ])
                for i, value in enumerate(outs):
                    acc[pl.ds(pl.multiple_of(i * TILES + g * 8, 8), 8), lanes] = value
            return carry

        lax.fori_loop(0, GROUPS, add, 0)
        return carry

    lax.fori_loop(0, SUB, window, 0)

    def owners_out(b, carry):
        lines = pick[pl.ds(pl.multiple_of(b * 64, 64), 64), :]
        for l in range(CH // 256):
            part = acc[:, l * 256:(l + 1) * 256]
            high = part.astype(jnp.bfloat16)
            rest = part - high.astype(jnp.float32)
            mid = rest.astype(jnp.bfloat16)
            low = (rest - mid.astype(jnp.float32)).astype(jnp.bfloat16)
            got = jnp.dot(lines, high, preferred_element_type=jnp.float32)
            got += jnp.dot(lines, mid, preferred_element_type=jnp.float32)
            got += jnp.dot(lines, low, preferred_element_type=jnp.float32)
            lsend[0:4, :, l * 256:(l + 1) * 256] = got.reshape(4, 16, 256)

        for t in range(8):
            rows = lsend[t // 2, (t % 2) * 8:(t % 2) * 8 + 8, :]
            peak = jnp.zeros((8, 128), jnp.float32)
            for l in range(CH // 128):
                peak = jnp.maximum(peak, jnp.abs(rows[:, l * 128:(l + 1) * 128]))
            code = code_of(peak)
            scale = jnp.exp(code * (-1.0 / FINE)) * TOP
            fbuf[b * 8 + t, :, CH:] = code.astype(jnp.int32).astype(jnp.int16)
            for l in range(CH // 128):
                value = jnp.round(rows[:, l * 128:(l + 1) * 128] * scale)
                fbuf[b * 8 + t, :, l * 128:(l + 1) * 128] = value.astype(jnp.int32).astype(jnp.int16)
        return carry

    lax.fori_loop(0, N_TM // 8, owners_out, 0)

    def relative(i):
        return lax.rem(i, 4), far_first(i // 8), lax.rem(i // 4, 2)

    def f_copy(i):
        dx, dz, dc = relative(i)
        target = (lax.rem(my_x + dx, NX) * NZ + lax.rem(my_z + dz, NZ)) * NC + lax.rem(core + dc, NC)
        return pltpu.make_async_remote_copy(
            src_ref=fbuf.at[target], dst_ref=fbuf.at[N_TM + i],
            send_sem=f_send.at[i], recv_sem=f_recv.at[i],
            device_id=(target, my_y), device_id_type=MESH)

    SELF = N_TM - 8

    def f_start(i, carry):
        @pl.when(i != SELF)
        def _():
            f_copy(i).start()

        return carry

    lax.fori_loop(0, N_TM, f_start, 0)

    def l_copy(piece, to, turn):
        return pltpu.make_async_remote_copy(
            src_ref=lsend.at[piece], dst_ref=lrecv.at[turn, lax.rem(piece, 4)],
            send_sem=l_send.at[piece], recv_sem=l_recv.at[turn, lax.rem(piece, 4)],
            device_id=(me, to), device_id_type=MESH)

    col = lax.broadcasted_iota(jnp.int32, (16, 128), 1)
    row = lax.broadcasted_iota(jnp.int32, (16, 128), 0)

    def owners_in(p, carry):
        _, dz, dc = relative(p * 4)
        from_z = lax.rem(my_z - dz + NZ, NZ)
        from_core = lax.rem(core + dc, NC)
        piece = from_core * NZ + from_z
        parts = []
        start = jnp.zeros((16, 128), jnp.int32)
        for dx in range(NX):
            i = p * 4 + dx
            if dx == 0:
                @pl.when(i != SELF)
                def _():
                    f_copy(i).wait_recv()

                alone = jnp.where(i == SELF, 1, 0)
                at = alone * me + (1 - alone) * (N_TM + i)
            else:
                f_copy(i).wait_recv()
                at = N_TM + i
            code = fbuf[at, :, CH:].astype(jnp.int32).astype(jnp.float32)
            scale = jnp.exp(code * (1.0 / FINE)) * (1.0 / TOP)
            value = fbuf[at, :, 0:CH].astype(jnp.int32).astype(jnp.float32)
            parts.append(value * jnp.concatenate([scale] * (CH // 128), axis=1))
            from_day = day(lax.rem(my_x - dx + NX, NX) * NZ + from_z - (LONG - from_core))
            start = jnp.where(lax.shift_right_logical(col, 3) == dx, jnp.concatenate([from_day] * 2, axis=0), start)
        same = (lax.shift_right_logical(col, 2) & 1) == lax.shift_right_logical(row, 3)
        spread = jnp.where(same & (((start + (col & 3)) & 7) == (row & 7)), 1.0, 0.0)[:, 0:32]
        value = jnp.concatenate(parts, axis=0)
        means = jnp.dot(spread, value, preferred_element_type=jnp.float32,
                        precision=lax.Precision.HIGHEST) * (1.0 / 24.0)
        lanes = pl.ds(pl.multiple_of(piece * CH, CH), CH)
        daily[0, 0, :, lanes] = means[0:8]
        daily[0, 1, :, lanes] = means[8:16]
        lsend[piece] = means * jnp.concatenate([share] * (CH // 128), axis=1)
        to = piece // 4
        turn = lax.rem(to - my_y + NY, NY)

        @pl.when(turn > 0)
        def _():
            l_copy(piece, to, turn).start()

        return carry

    lax.fori_loop(0, NZ * NC, owners_in, 0)

    for s in range(4):
        total = lsend[my_y * 4 + s]
        for turn in range(1, NY):
            l_copy(my_y * 4 + s, my_y, turn).wait_recv()
            total += lrecv[turn, s]
        column[0, :, s * CH:(s + 1) * CH] = total[0:8]
        column[1, :, s * CH:(s + 1) * CH] = total[8:16]

    def drain_pair(n, carry):
        pair_copy(n).wait_send()
        return carry

    def drain_length(r, carry):
        length_copy(r).wait_send()
        return carry

    def drain_f(i, carry):
        @pl.when(i != SELF)
        def _():
            f_copy(i).wait_send()

        return carry

    def drain_l(piece, carry):
        to = piece // 4
        turn = lax.rem(to - my_y + NY, NY)

        @pl.when(turn > 0)
        def _():
            l_copy(piece, to, turn).wait_send()

        return carry

    lax.fori_loop(0, NZ, drain_pair, 0)
    lax.fori_loop(1, N_TM, drain_length, 0)
    for s in range(SUB):
        for n in range(1, LONG + 1):
            link(False, n, s).wait_send()
        for n in range(1, SHORT + 1):
            link(True, n, s).wait_send()
    lax.fori_loop(0, N_TM, drain_f, 0)
    lax.fori_loop(0, NZ * NC, drain_l, 0)


def slot_of(owners):
    ids = jnp.arange(TILES, dtype=jnp.int32)
    earlier = (owners[None, :] == owners[:, None]) & (ids[None, :] < ids[:, None])
    return owners * MAXT + jnp.sum(earlier.astype(jnp.int32), axis=1)


def local(fields, lengths, owners, thickness):
    place = jnp.tile(slot_of(owners), WIN)[None, :]
    dma = pltpu.SemaphoreType.DMA
    steps = LONG + SHORT
    two, three = 2 * GROUPS * CW + 128, 3 * GROUPS * CW + 128
    return pl.pallas_call(
        kernel,
        out_shape=(
            jax.ShapeDtypeStruct((1, MAXT, DAYS, CELLS), jnp.float32),
            jax.ShapeDtypeStruct((MAXT, DAYS, CELLS // NY), jnp.float32),
        ),
        in_specs=[
            pl.BlockSpec(memory_space=pl.ANY),
            pl.BlockSpec(memory_space=pltpu.SMEM),
            pl.BlockSpec(memory_space=pltpu.SMEM),
            pl.BlockSpec(memory_space=pltpu.VMEM),
        ],
        out_specs=(pl.BlockSpec(memory_space=pltpu.VMEM), pl.BlockSpec(memory_space=pltpu.VMEM)),
        scratch_shapes=[
            pltpu.VMEM((NZ, CAP, TILES, CH), jnp.bfloat16),
            pltpu.VMEM((NZ, CAP, TILES, CH), jnp.bfloat16),
            pltpu.VMEM((N_TM, 128), jnp.int32),
            pltpu.VMEM((N_TM, 128), jnp.int32),
            pltpu.VMEM((MAXT * N_TM * WIN, WIN * TILES), jnp.bfloat16),
            pltpu.VMEM((3 * GROUPS, 8, CW), jnp.float32),
            pltpu.VMEM((6, SUB, 8, two), jnp.int16),
            pltpu.VMEM((6, SUB, 8, two), jnp.int16),
            pltpu.VMEM((SUB, 8, three), jnp.int16),
            pltpu.VMEM((SUB, 8, three), jnp.int16),
            pltpu.VMEM((WIN * TILES, CH), jnp.float32),
            pltpu.VMEM((2 * N_TM, 8, FW), jnp.int16),
            pltpu.VMEM((NZ * NC, 16, CH), jnp.float32),
            pltpu.VMEM((NY, 4, 16, CH), jnp.float32),
            dma((NZ,)), dma((NZ,)), dma((NZ,)), dma((N_TM,)), dma((N_TM,)),
            dma((steps, SUB)), dma((steps, SUB)),
            dma((N_TM,)), dma((N_TM,)), dma((NZ * NC,)), dma((NY, 4)),
        ],
        compiler_params=pltpu.CompilerParams(collective_id=0, has_side_effects=True),
    )(fields, lengths, thickness, place)


def solution(mesh):
    placed = (P("lev", "tm", None, None), P("tm"), P(), P())
    return jax.shard_map(
        local,
        mesh=mesh,
        in_specs=placed,
        out_specs=(P("lev", "tm", None, None), P("tm", None, "lev")),
        check_vma=False,
    )
```

time: 163 us -> 103 us (0.63)
  blocking collectives: 20.7 us -> 0 us
  Pallas kernels: 114 us -> 94.4 us
  local copies, waits for them, and re-layouts: 13.1 us -> 4.58 us
  other arithmetic: 9.66 us -> 1.58 us
    unnamed x1 -> x0, blocking collectives: 20.7 us -> none
    pallas_call x1, Pallas kernels: 114 us -> 94.4 us  [local(): pl.pallas_call(kernel, out_shape=(jax.ShapeDtypeStruct((1, MAXT, DAYS, CE...]
    select_n x9 -> x0, other arithmetic: 3.41 us -> none  [the longest x1 2.54 us: local(): cols // 4 % 2]
    gather x5 -> x0, local copies, waits for them, and re-layouts: 3.17 us -> none  [the longest x2 1.25 us: local(): day = plane_day[from_x][cols // 8] + cols % 4]
    dynamic_slice x3 -> x0, local copies, waits for them, and re-layouts: 2.41 us -> none  [the longest x1 1.24 us: local(): frac = (thickness[lax.axis_index('lev')] / jnp.sum(thickness)).reshape(1)]
    unnamed x5 -> x2, local copies, waits for them, and re-layouts: 5.95 us -> 3.93 us
    convert_element_type x4 -> x0, other arithmetic: 1.98 us -> none  [the longest x1 1.23 us: local(): pick = jnp.concatenate([taken & (lines % XSLOTS == s)[:, None] for s in r...]
where the time goes in v2:
time: 103 us; the launch traced here: 102 us
  Pallas kernels  94.4 us (92%)
  local copies, waits for them, and re-layouts  4.58 us (4%)
  other arithmetic  1.58 us (2%)
  between operations  1.29 us (1%)
    pallas_call x1, Pallas kernels, local(): pl.pallas_call(kernel, out_shape=(jax.ShapeDtypeStruct((1, MAXT, DAYS, CE...  94.4 us
    unnamed x2, local copies, waits for them, and re-layouts  3.93 us

profile of v2, /device:TPU:1, one launch (start us, length us, event | category | flops | bytes accessed | tf_op | source)
XLA Modules:
  0.0 101.9 jit_solution(6315762300065273271)
XLA Ops:
  1.3 0.9 convert_reduce_fusion
  2.2 0.7 multiply_add_fusion
  2.9 0.6 broadcast_in_dim_tile.3.place
  3.5 94.4 %shard_map.59 = (f32[1,2,8,16384]{3,2,1,0:T(8,128)}, f32[2,8,4096]{2,1,0:T(8,128)}) custom-call(bf16[1,4,72,16384]{3,2,1,0:T(8,128)(2,1)} %fields.1, s32[1]{0:T(128)S(6)} %copy.8.length, f32[4]{0:T(128)} %thickness.1, s32[1,288]{1,0:T(1,128)} %broadcast_in_dim_tile.3.place), custom_call_target="tpu_custom_call" | custom-call | tf_op jit(solution)/shard_map/pallas_call | solution.py:439
  97.9 2.3 %copy.9 = f32[1,2,8,16384]{3,2,1,0:T(8,128)} copy(f32[1,2,8,16384]{3,2,1,0:T(8,128)} %get-tuple-element.4) | data formatting | bytes 2097152
  100.2 1.7 %copy.10 = f32[2,8,4096]{2,1,0:T(8,128)} copy(f32[2,8,4096]{2,1,0:T(8,128)} %get-tuple-element.5) | data formatting | bytes 524288
  (1 shorter events, 0.0 us)
